TPU v7x, 32 devices: a whole 2x2x4 slice. The times are simulated.
32 devices in a mesh: inter: 4 (over y, x), intra: 8 (over z, core).
Axes of the slice: x: 2, y: 2, z: 4, core: 2. Of those that a mesh axis runs over, the one named last changes fastest.
Arguments:
- layer_input: bfloat16 [4096, 4608], P(('inter', 'intra')), may hold values from -80 to 80
- norm_gain: bfloat16 [4608], P('intra'), may hold values from 0.5 to 1.5
- kv_weight: bfloat16 [4608, 128], P('intra'), may hold values from -0.09375 to 0.09375
- kv_cotangent: bfloat16 [4096, 128], P(('inter', 'intra')), may hold values from -24 to 24
Outputs:
- input_grad: bfloat16 [4096, 4608], P(('inter', 'intra'))
- weight_grad: float32 [4608, 128], P(('inter', 'intra'))
- gain_grad: float32 [4608], P(('inter', 'intra'))
All inputs are finite; a program needn't handle non-finite values.
Results may differ from a plain program's by a relative error of at most 0.0029.
Values may be sent and summed in bfloat16 or wider, within the bound.
A program may use at most 64 MiB of HBM per device.

v0:
```python
import jax
import jax.numpy as jnp
from jax import lax
from jax.sharding import PartitionSpec as P

EPS = 1e-05


def on_device(layer_input, norm_gain, kv_weight, kv_cotangent):
    weight_all, gain_all = (
        lax.all_gather(kv_weight, "intra", axis=0, tiled=True),
        lax.all_gather(norm_gain, "intra", axis=0, tiled=True),
    )
    gain_wide = gain_all.astype(jnp.float32)
    widened = layer_input.astype(jnp.float32)
    inverse_rms = lax.rsqrt(jnp.mean(widened * widened, axis=1, keepdims=True) + EPS)
    normal_rows = widened * inverse_rms
    normed = (normal_rows * gain_wide).astype(jnp.bfloat16)
    weight_term = lax.dot_general(
        normed, kv_cotangent, (((0,), (0,)), ((), ())), preferred_element_type=jnp.float32
    )
    feature_grad = lax.dot_general(
        kv_cotangent, weight_all, (((1,), (1,)), ((), ())), preferred_element_type=jnp.float32
    )
    gain_term = jnp.sum(feature_grad * normal_rows, axis=0)
    outer_count = lax.axis_size("inter")
    inner_count = lax.axis_size("intra")
    devices = outer_count * inner_count
    part_weight, part_gain = (
        lax.psum_scatter(weight_term, "inter", scatter_dimension=0, tiled=True),
        lax.psum_scatter(gain_term, "inter", scatter_dimension=0, tiled=True),
    )
    weight_grad, gain_grad = (
        lax.psum_scatter(part_weight, "intra", scatter_dimension=0, tiled=True),
        lax.psum_scatter(part_gain, "intra", scatter_dimension=0, tiled=True),
    )
    scaled_grad = feature_grad * gain_wide
    centre = jnp.mean(scaled_grad * normal_rows, axis=1, keepdims=True)
    input_grad = (inverse_rms * (scaled_grad - normal_rows * centre)).astype(jnp.bfloat16)
    return (input_grad, weight_grad / float(devices), gain_grad / float(devices))


def solution(mesh):
    return jax.shard_map(
        on_device,
        mesh=mesh,
        in_specs=(
            P(("inter", "intra"), None),
            P("intra"),
            P("intra", None),
            P(("inter", "intra"), None),
        ),
        out_specs=(P(("inter", "intra"), None), P(("inter", "intra"), None), P(("inter", "intra"))),
        check_vma=False,
    )
```

profile of v0, /device:TPU:0, one launch (start us, length us, event | category | flops | bytes accessed | tf_op | source)
XLA Modules:
  0.0 124.3 jit_solution(481435414101558921)
XLA Ops:
  8.0 0.0 copy-start
  8.0 0.0 all-gather.2.cloned.1.call-start
  8.1 0.7 all-gather.2.cloned.1.call-update
  8.7 0.0 reduce-scatter.3.cloned.1.call-start
  8.8 1.3 %fusion.15 = (u32[1]{0:T(128)}, u32[1]{0:T(128)}) fusion(u32[32]{0:T(128)} %constant.15, u32[]{:T(128)S(6)} %add.24, u32[]{:T(128)S(6)} %add.21), kind=kLoop, calls=%fused_computation.20 | loop fusion | bytes 24
  10.8 0.9 dynamic-update-slice
  11.7 30.6 %all-reduce = bf16[4608]{0:T(1024)(128)(2,1)S(1)} all-reduce(bf16[4608]{0:T(1024)(128)(2,1)S(1)} %dynamic-update-slice), channel_id=1, replica_groups=mesh['inter'=4,'intra'=8] {'intra'}, use_global_device_ids=true, to_apply=%add | all-reduce | flops 4608 | bytes 18432
  42.3 1.6 %fusion.10 = f32[128]{0:T(128)S(1)} fusion(bf16[128,4608]{1,0:T(8,128)(2,1)} %param.4), kind=kLoop, calls=%fused_computation.12 | loop fusion | flops 1769344 | bytes 1180160 | tf_op jit(solution)/shard_map/reduce_sum | solution.py:16
  43.9 0.0 copy-done
  43.9 0.0 copy-start.2
  43.9 0.0 copy-start.1
  43.9 3.3 %fusion.11 = f32[4608,128]{1,0:T(8,128)} fusion(bf16[128,128]{1,0:T(8,128)(2,1)S(1)} %copy-done, bf16[128,4608]{1,0:T(8,128)(2,1)} %param.4, f32[4608]{0:T(1024)S(1)} %convert_element_type.13, f32[128]{0:T(128)S(1)} %add_rsqrt_fusion), kind=kOutput, calls=%fused_computation.13 | convolution fusion | flops 153354240 | bytes 3590656 | tf_op jit(solution)/shard_map/dot_general | solution.py:19
  47.2 0.0 reduce-scatter.3.cloned.1.call-update
  47.3 0.0 reduce-scatter.5.cloned.1.call-start
  47.3 0.0 copy-done.2
  47.3 0.6 dynamic-slice.1
  49.2 0.0 all-gather.2.cloned.1.call-done
  49.2 0.0 copy-done.1
  49.2 3.4 %fusion.9 = (f32[4608]{0:T(1024)S(1)}, f32[128]{0:T(128)S(1)}, f32[128,4608]{1,0:T(8,128)}) fusion(bf16[128,4608]{1,0:T(8,128)(2,1)S(1)} %copy-done.1, f32[128]{0:T(128)S(1)} %add_rsqrt_fusion, f32[4608]{0:T(1024)S(1)} %convert_element_type.13, bf16[128,128]{1,0:T(8,128)(2,1)S(1)} %copy-done, bf16[4608,128]{1,0:T(8,128)(2,1)} %all-gather.2.cloned.1.call-done), kind=kOutput, calls=%fused_computation.11 | convolution fusion | flops 155118976 | bytes 4789248 | tf_op jit(solution)/shard_map/dot_general | solution.py:22
  52.6 17.4 %all-reduce.1 = f32[4608]{0:T(1024)S(1)} all-reduce(f32[4608]{0:T(1024)S(1)} %get-tuple-element.3), channel_id=4, replica_groups=mesh['inter'=4,'intra'=8] {'inter'}, use_global_device_ids=true, to_apply=%region_5.0.clone | all-reduce | flops 4608 | bytes 36864
  70.0 0.1 dynamic-slice.2
  70.1 13.9 %all-reduce.2 = f32[1152]{0:T(1024)S(1)} all-reduce(f32[1152]{0:T(1024)S(1)} %dynamic-slice.2), channel_id=5, replica_groups=mesh['inter'=4,'intra'=8] {'intra'}, use_global_device_ids=true, to_apply=%region_6.0.clone | all-reduce | flops 1152 | bytes 9216
  84.0 0.6 dynamic-slice_multiply_fusion
  84.6 0.0 reduce-scatter.3.cloned.1.call-done
  84.6 0.0 reduce-scatter.5.cloned.1.call-update
  84.7 3.3 %fusion.7 = bf16[128,4608]{1,0:T(8,128)(2,1)} fusion(bf16[128,4608]{1,0:T(8,128)(2,1)S(1)} %copy-done.1, f32[128,4608]{1,0:T(8,128)} %get-tuple-element.7, f32[128]{0:T(128)S(1)} %broadcast_multiply_fusion.1, f32[4608]{0:T(1024)S(1)} %convert_element_type.13, f32[128]{0:T(128)S(1)} %add_rsqrt_fusion), kind=kLoop, calls=%fused_computation.9 | loop fusion | flops 4128768 | bytes 4738048 | tf_op jit(solution)/shard_map/convert_element_type | solution.py:39
  87.9 27.4 %reduce-scatter.5.cloned.1.call-done = f32[144,128]{1,0:T(8,128)} async-done(((f32[1152,128]{1,0:T(8,128)}), f32[144,128]{1,0:T(8,128)}) %reduce-scatter.5.cloned.1.call-update) | async-done | bytes 73744 | tf_op jit(solution)/shard_map/reduce_scatter | solution.py:34
  115.3 1.5 %broadcast_multiply_fusion = f32[144,128]{1,0:T(8,128)} fusion(f32[144,128]{1,0:T(8,128)} %reduce-scatter.5.cloned.1.call-done), kind=kLoop, calls=%fused_computation.16 | loop fusion | flops 18432 | bytes 147456 | tf_op jit(solution)/shard_map/div | solution.py:40
  (4 shorter events, 0.0 us)
Async XLA Ops:
  8.0 35.9 %copy-start = (bf16[128,128]{1,0:T(8,128)(2,1)S(1)}, bf16[128,128]{1,0:T(8,128)(2,1)}, u32[]{:S(2)}) copy-start(bf16[128,128]{1,0:T(8,128)(2,1)} %param.7) | copy-start | bytes 98308
  8.0 41.2 %all-gather.2.cloned.1.call-start = ((), (), s32[]{:S(2)}) async-start(), calls=%async_computation.2 | async-start | bytes 1327104 | tf_op jit(solution)/shard_map/all_gather | solution.py:11
  8.7 75.9 %reduce-scatter.3.cloned.1.call-start = ((), (), s32[]{:S(2)}) async-start(), calls=%async_computation.3 | async-start | bytes 2949120 | tf_op jit(solution)/shard_map/reduce_scatter | solution.py:30
  43.9 3.4 %copy-start.2 = (u32[32]{0:T(128)S(1)}, u32[32]{0:T(128)}, u32[]{:S(2)}) copy-start(u32[32]{0:T(128)} %constant.21) | copy-start | bytes 388
  43.9 5.4 %copy-start.1 = (bf16[128,4608]{1,0:T(8,128)(2,1)S(1)}, bf16[128,4608]{1,0:T(8,128)(2,1)}, u32[]{:S(2)}) copy-start(bf16[128,4608]{1,0:T(8,128)(2,1)} %param.4) | copy-start | bytes 3538948
  47.3 68.1 %reduce-scatter.5.cloned.1.call-start = ((), (), s32[]{:S(2)}) async-start(), calls=%async_computation.4 | async-start | bytes 663552 | tf_op jit(solution)/shard_map/reduce_scatter | solution.py:34
Sparse Core Ops, SparseCore 0:
  10.5 25.6 all-gather.1
  84.8 30.4 reduce-scatter.4
Sparse Core Ops, SparseCore 1:
  47.3 36.2 reduce-scatter.2
where the time goes:
time: 125 us; the launch traced here: 124 us
  blocking collectives  61.9 us (50%)
  waiting for transfers between devices  28.1 us (22%)
  between operations  17.5 us (14%)
  other arithmetic  7.03 us (6%)
  matrix products  6.72 us (5%)
  local copies, waits for them, and re-layouts  2.89 us (2%)
    unnamed x3, blocking collectives  61.9 us
    reduce_scatter x1, waiting for transfers between devices, on_device(): lax.psum_scatter(part_weight, 'intra', scatter_dimension=0, tiled=True)  27.4 us
    dot_general x1, matrix products, on_device(): lax.dot_general(kv_cotangent, weight_all, (((1,), (1,)), ((), ())), prefe...  3.38 us
    dot_general x1, matrix products, on_device(): lax.dot_general(normed, kv_cotangent, (((0,), (0,)), ((), ())), preferred...  3.34 us
    convert_element_type x1, other arithmetic, on_device(): (inverse_rms * (scaled_grad - normal_rows * centre)).astype(jnp.bfloat16)  3.27 us
    unnamed x11, local copies, waits for them, and re-layouts  2.89 us
  transfers between devices with their start and end apart: 3, of which 1 were waited for; matrix products, arithmetic and copies ran while one was open for 12% of the time, Pallas kernels for 0%

commit v1 on v0

--- a/solution.py
+++ b/solution.py
@@ -1,12 +1,223 @@
+import functools
+
 import jax
 import jax.numpy as jnp
 from jax import lax
+from jax.experimental import pallas as pl
+from jax.experimental.pallas import tpu as pltpu
 from jax.sharding import PartitionSpec as P
 
 EPS = 1e-05
-
-
-def on_device(layer_input, norm_gain, kv_weight, kv_cotangent):
+MESH = pl.DeviceIdType.MESH
+LANES = 128
+
+
+def fused_kernel(m, n, x_hbm, gwin_ref, w_ref, cot_ref, dx_hbm, wg_ref, gg_ref,
+                 x_ref, gbuf, gfull, wall, t_ref, pr, xs, xr, u_ref, zs, zr, sref, dxv,
+                 x_sem, dx_sem, g_send, g_recv, wz_send, wz_recv, wf_send, wf_recv,
+                 p_send, p_recv, x_send, x_recv, z_send, z_recv):
+    a, j = lax.axis_index("inter"), lax.axis_index("intra")
+    z, c = j // 2, lax.rem(j, 2)
+    other = 1 - c
+    chips = n // 2
+    tokens, features = x_ref.shape
+    quarter, pair, shard = features // m, features // chips, features // n
+    block = quarter // n
+    window = gwin_ref.shape[1]
+    low = pair - window
+
+    barrier = pltpu.get_barrier_semaphore()
+    for k in range(1, n):
+        pl.semaphore_signal(barrier, inc=1, device_id=(a, lax.rem(j + k, n)), device_id_type=MESH)
+    for k in range(1, m):
+        pl.semaphore_signal(barrier, inc=1, device_id=(lax.rem(a + k, m), j), device_id_type=MESH)
+    x_copy = pltpu.make_async_copy(x_hbm, x_ref, x_sem)
+    x_copy.start()
+    gbuf[j] = gwin_ref[...]
+    wall[pl.ds(pl.multiple_of(j * shard, 16), shard), :] = w_ref[...]
+    pl.semaphore_wait(barrier, n - 1 + m - 1)
+
+    def send(src, dst, s_sem, r_sem, to):
+        copy = pltpu.make_async_remote_copy(src_ref=src, dst_ref=dst, send_sem=s_sem, recv_sem=r_sem,
+                                            device_id=to, device_id_type=MESH)
+        copy.start()
+        return copy
+
+    started = []
+    gains = []
+    for k in range(1, n):
+        gains.append(send(gwin_ref, gbuf.at[j], g_send.at[k - 1], g_recv.at[k - 1], (a, lax.rem(j + k, n))))
+
+    def rows_of(owner):
+        return wall.at[pl.ds(pl.multiple_of(owner * shard, 16), shard), :]
+
+    mate = (a, 2 * z + other)
+    w_z = []
+    for k in range(1, chips):
+        to = lax.rem(z + k, chips)
+        w_z.append(send(w_ref, rows_of(j), wz_send.at[k - 1], wz_recv.at[k - 1], (a, 2 * to + c)))
+    w_f = [send(w_ref, rows_of(j), wf_send.at[0], wf_recv.at[0], mate)]
+
+    x_copy.wait()
+    wide = x_ref[...].astype(jnp.float32)
+    inv = lax.rsqrt(jnp.mean(wide * wide, axis=1, keepdims=True) + EPS)
+
+    for copy in gains:
+        copy.wait_recv()
+    for q in range(chips):
+        even, odd = gbuf[2 * q], gbuf[2 * q + 1]
+        base = q * pair
+        gfull[:, base:base + low] = even[:, :low]
+        gfull[:, base + low:base + window] = even[:, low:] + odd[:, :window - low]
+        gfull[:, base + window:base + pair] = odd[:, window - low:]
+
+    order = list(range(1, m)) + [0]
+    p_copies, x_copies = {}, []
+    for step in range(m + 1):
+        if step < m:
+            k = order[step]
+            part = lax.rem(a + k, m)
+            cols = pl.ds(pl.multiple_of(part * quarter, LANES), quarter)
+            normed = (x_ref[:, cols].astype(jnp.float32) * inv * gfull[:, cols]).astype(jnp.bfloat16)
+            term = lax.dot_general(normed, cot_ref[...], (((0,), (0,)), ((), ())),
+                                   preferred_element_type=jnp.float32)
+            for q in range(chips):
+                for core in range(2):
+                    at = (2 * q + core) * block
+                    t_ref[k, core, q * block:(q + 1) * block, :] = term[at:at + block, :]
+            p_copies[k] = send(t_ref.at[k, other], pr.at[k], p_send.at[k], p_recv.at[k], mate)
+        if step >= 1:
+            k = order[step - 1]
+            p_copies[k].wait_recv()
+            if k:
+                xs[k - 1] = (t_ref[k, c] + pr[k]).astype(jnp.bfloat16)
+                x_copies.append(send(xs.at[k - 1], xr.at[k - 1], x_send.at[k - 1], x_recv.at[k - 1],
+                                     (lax.rem(a + k, m), j)))
+            else:
+                u_ref[...] = t_ref[0, c] + pr[0]
+
+    for k in range(1, chips):
+        w_z[k - 1].wait_recv()
+        owner = 2 * lax.rem(z - k + chips, chips) + c
+        w_f.append(send(rows_of(owner), rows_of(owner), wf_send.at[k], wf_recv.at[k], mate))
+
+    acc = jnp.zeros((tokens, 1), jnp.float32)
+
+    def feature(k, acc):
+        w_f[k].wait_recv()
+        q = lax.rem(z - k + chips, chips)
+        cols = pl.ds(pl.multiple_of(q * pair, LANES), pair)
+        grad = lax.dot_general(cot_ref[...], wall[cols, :], (((1,), (1,)), ((), ())),
+                               preferred_element_type=jnp.float32)
+        scaled = grad * gfull[:, cols]
+        sref[:, cols] = scaled
+        normal = x_ref[:, cols].astype(jnp.float32) * inv
+        return acc + jnp.sum(scaled * normal, axis=1, keepdims=True)
+
+    for copy in x_copies:
+        copy.wait_recv()
+    total = u_ref[...]
+    for k in range(1, m):
+        total = total + xr[k - 1].astype(jnp.float32)
+    u_ref[...] = total
+    z_copies = []
+    for k in range(1, chips):
+        to = lax.rem(z + k, chips)
+        rows = pl.ds(pl.multiple_of(to * block, 16), block)
+        zs[k - 1] = u_ref[rows, :].astype(jnp.bfloat16)
+        z_copies.append(send(zs.at[k - 1], zr.at[k - 1], z_send.at[k - 1], z_recv.at[k - 1], (a, 2 * to + c)))
+
+    for k in range(chips):
+        acc = feature(k, acc)
+    centre = acc * (1.0 / features)
+    dx_copies = []
+    for q in range(m):
+        cols = slice(q * quarter, (q + 1) * quarter)
+        normal = x_ref[:, cols].astype(jnp.float32) * inv
+        dxv[:, cols] = (inv * (sref[:, cols] - normal * centre)).astype(jnp.bfloat16)
+        copy = pltpu.make_async_copy(dxv.at[:, cols], dx_hbm.at[:, cols], dx_sem.at[q])
+        copy.start()
+        dx_copies.append(copy)
+
+    cols = pl.ds(pl.multiple_of(a * quarter, LANES), quarter)
+    lane = lax.broadcasted_iota(jnp.int32, (block, quarter), 1)
+    row = lax.broadcasted_iota(jnp.int32, (block, quarter), 0)
+    gain = jnp.sum(jnp.where(lane == row + j * block, gfull[:, cols], 0.0), axis=1, keepdims=True)
+    own = wall[pl.ds(pl.multiple_of((a * n + j) * block, 16), block), :].astype(jnp.float32) / gain
+
+    for copy in z_copies:
+        copy.wait_recv()
+    final = u_ref[pl.ds(pl.multiple_of(z * block, 16), block), :]
+    for k in range(1, chips):
+        final = final + zr[k - 1].astype(jnp.float32)
+    final = final / float(m * n)
+    wg_ref[...] = final
+    ones = jnp.ones((8, final.shape[1]), jnp.float32)
+    sums = lax.dot_general(ones, final * own, (((1,), (1,)), ((), ())),
+                           precision=lax.Precision.HIGHEST, preferred_element_type=jnp.float32)
+    gg_ref[...] = sums[0:1, :]
+
+    for copy in dx_copies:
+        copy.wait()
+    for copy in gains + w_z + w_f + list(p_copies.values()) + x_copies + z_copies:
+        copy.wait_send()
+
+
+def fused(layer_input, norm_gain, kv_weight, kv_cotangent):
+    m, n = lax.axis_size("inter"), lax.axis_size("intra")
+    tokens, features = layer_input.shape
+    width = kv_weight.shape[1]
+    shard = kv_weight.shape[0]
+    chips = n // 2
+    quarter, pair = features // m, 2 * shard
+    block = features // (m * n)
+    half = features // m // 2
+    window = pair - shard // LANES * LANES
+    lead = window - shard
+    wide = norm_gain.astype(jnp.float32)
+    odd = lax.rem(lax.axis_index("intra"), 2) == 1
+    gwin = jnp.where(odd, jnp.pad(wide, (lead, 0)), jnp.pad(wide, (0, lead))).reshape(1, window)
+    f32, bf16 = jnp.float32, jnp.bfloat16
+    dma = pltpu.SemaphoreType.DMA
+    vmem = pl.BlockSpec(memory_space=pltpu.VMEM)
+    hbm = pl.BlockSpec(memory_space=pl.ANY)
+    dx, wg, gg = pl.pallas_call(
+        functools.partial(fused_kernel, m, n),
+        out_shape=(
+            jax.ShapeDtypeStruct((tokens, features), bf16),
+            jax.ShapeDtypeStruct((block, width), f32),
+            jax.ShapeDtypeStruct((1, block), f32),
+        ),
+        in_specs=[hbm, vmem, vmem, vmem],
+        out_specs=(hbm, vmem, vmem),
+        scratch_shapes=[
+            pltpu.VMEM((tokens, features), bf16),
+            pltpu.VMEM((n, 1, window), f32),
+            pltpu.VMEM((1, features), f32),
+            pltpu.VMEM((features, width), bf16),
+            pltpu.VMEM((m, 2, half, width), f32),
+            pltpu.VMEM((m, half, width), f32),
+            pltpu.VMEM((m - 1, half, width), bf16),
+            pltpu.VMEM((m - 1, half, width), bf16),
+            pltpu.VMEM((half, width), f32),
+            pltpu.VMEM((chips - 1, block, width), bf16),
+            pltpu.VMEM((chips - 1, block, width), bf16),
+            pltpu.VMEM((tokens, features), f32),
+            pltpu.VMEM((tokens, features), bf16),
+            dma(()), dma((m,)),
+            dma((n - 1,)), dma((n - 1,)),
+            dma((chips - 1,)), dma((chips - 1,)),
+            dma((chips,)), dma((chips,)),
+            dma((m,)), dma((m,)),
+            dma((m - 1,)), dma((m - 1,)),
+            dma((chips - 1,)), dma((chips - 1,)),
+        ],
+        compiler_params=pltpu.CompilerParams(collective_id=0, has_side_effects=True),
+    )(layer_input, gwin, kv_weight, kv_cotangent)
+    return dx, wg, gg.reshape(block)
+
+
+def plain(layer_input, norm_gain, kv_weight, kv_cotangent):
     weight_all, gain_all = (
         lax.all_gather(kv_weight, "intra", axis=0, tiled=True),
         lax.all_gather(norm_gain, "intra", axis=0, tiled=True),
@@ -38,6 +249,21 @@
     centre = jnp.mean(scaled_grad * normal_rows, axis=1, keepdims=True)
     input_grad = (inverse_rms * (scaled_grad - normal_rows * centre)).astype(jnp.bfloat16)
     return (input_grad, weight_grad / float(devices), gain_grad / float(devices))
+
+
+def on_device(layer_input, norm_gain, kv_weight, kv_cotangent):
+    m, n = lax.axis_size("inter"), lax.axis_size("intra")
+    features = layer_input.shape[1]
+    fits = (
+        n % 2 == 0 and n > 2 and m > 1
+        and features % (16 * m * n) == 0
+        and features % (LANES * m) == 0
+        and 2 * features % (LANES * n) == 0
+        and layer_input.shape[0] % 16 == 0
+        and kv_weight.shape[1] % LANES == 0
+    )
+    path = fused if fits else plain
+    return path(layer_input, norm_gain, kv_weight, kv_cotangent)
 
 
 def solution(mesh):

time: 125 us -> 34.6 us (0.28)
  blocking collectives: 61.9 us -> 0 us
  Pallas kernels: 0 us -> 28.8 us
  waiting for transfers between devices: 28.1 us -> 0 us
  between operations: 17.5 us -> 0.66 us
  matrix products: 6.72 us -> 0 us
  other arithmetic: 7.03 us -> 0.76 us
  local copies, waits for them, and re-layouts: 2.89 us -> 4.18 us
    unnamed x3 -> x0, blocking collectives: 61.9 us -> none
    pallas_call x0 -> x1, Pallas kernels: none -> 28.8 us  [fused(): pl.pallas_call(functools.partial(fused_kernel, m, n), out_shape=(jax.Shap...]
    reduce_scatter x2 -> x0, waiting for transfers between devices: 27.4 us -> none  [the longest x1 27.4 us: on_device(): lax.psum_scatter(part_weight, 'intra', scatter_dimension=0, tiled=True)]
    dot_general x2 -> x0, matrix products: 6.72 us -> none  [the longest x1 3.38 us: on_device(): lax.dot_general(kv_cotangent, weight_all, (((1,), (1,)), ((), ())), prefe...]
    convert_element_type x2 -> x1, other arithmetic: 3.27 us -> 0.68 us  [fused(): wide = norm_gain.astype(jnp.float32)]
    div x3 -> x0, other arithmetic: 2.17 us -> none  [the longest x1 1.52 us: on_device(): weight_grad / float(devices)]
    reduce_sum x1 -> x0, other arithmetic: 1.58 us -> none  [on_device(): jnp.mean(widened * widened, axis=1, keepdims=True) + EPS]
    unnamed x11 -> x7, local copies, waits for them, and re-layouts: 2.89 us -> 3.59 us
  transfers between devices with their start and end apart: 3 -> 0, of which waited for: 1 -> 0; matrix products, arithmetic and copies ran while one was open for 12% -> 0% of each run, Pallas kernels for 0% -> 0%
where the time goes in v1:
time: 34.6 us; the launch traced here: 34.4 us
  Pallas kernels  28.8 us (83%)
  local copies, waits for them, and re-layouts  4.18 us (12%)
  other arithmetic  0.76 us (2%)
  between operations  0.66 us (2%)
    pallas_call x1, Pallas kernels, fused(): pl.pallas_call(functools.partial(fused_kernel, m, n), out_shape=(jax.Shap...  28.8 us
    unnamed x7, local copies, waits for them, and re-layouts  3.59 us

profile of v1, /device:TPU:0, one launch (start us, length us, event | category | flops | bytes accessed | tf_op | source)
XLA Modules:
  0.0 34.4 jit_solution(4299244660042539852)
XLA Ops:
  0.6 0.7 %convert_element_type.7 = f32[576]{0:T(1024)S(1)} convert(bf16[576]{0:T(1024)(128)(2,1)} %param.5) | non-fusion elementwise | flops 576 | bytes 3456 | tf_op jit(solution)/shard_map/convert_element_type | solution.py:177
  1.3 0.1 pad_select_fusion
  1.4 0.6 %reshape.12.gwin_ref = f32[1,640]{1,0:T(1,128)} reshape(f32[640]{0:T(1024)S(1)} %pad_select_fusion) | data formatting | bytes 5120 | tf_op jit(solution)/shard_map/reshape | solution.py:179
  2.0 28.8 %shard_map.67 = (bf16[128,4608]{1,0:T(8,128)(2,1)}, f32[144,128]{1,0:T(8,128)}, f32[1,144]{1,0:T(1,128)}) custom-call(bf16[128,4608]{1,0:T(8,128)(2,1)} %x_hbm.1, f32[1,640]{1,0:T(1,128)} %reshape.12.gwin_ref, bf16[576,128]{1,0:T(8,128)(2,1)} %w_ref.1, bf16[128,128]{1,0:T(8,128)(2,1)} %cot_ref.1), custom_call_target="tpu_custom_call" | custom-call | tf_op jit(solution)/shard_map/pallas_call | solution.py:184
  30.8 0.0 copy-start
  30.8 0.0 copy-start.1
  30.8 2.4 %copy.10 = bf16[128,4608]{1,0:T(8,128)(2,1)} copy(bf16[128,4608]{1,0:T(8,128)(2,1)} %get-tuple-element.12) | data formatting | bytes 2359296
  33.2 0.0 copy-done
  33.2 0.6 %copy.11 = f32[144,128]{1,0:T(8,128)} copy(f32[144,128]{1,0:T(8,128)S(1)} %copy-done) | data formatting | bytes 147456
  33.9 0.0 copy-done.1
  33.9 0.6 %copy.12 = f32[144]{0:T(256)} copy(f32[144]{0:T(256)S(1)} %bitcast.1) | data formatting | bytes 1152
Async XLA Ops:
  30.8 2.4 %copy-start = (f32[144,128]{1,0:T(8,128)S(1)}, f32[144,128]{1,0:T(8,128)}, u32[]{:S(2)}) copy-start(f32[144,128]{1,0:T(8,128)} %get-tuple-element.13) | copy-start | bytes 221188
  30.8 3.0 %copy-start.1 = (f32[1,144]{1,0:T(1,128)S(1)}, f32[1,144]{1,0:T(1,128)}, u32[]{:S(2)}) copy-start(f32[1,144]{1,0:T(1,128)} %get-tuple-element.8) | copy-start | bytes 1732

commit v2 on v1

--- a/solution.py
+++ b/solution.py
@@ -12,9 +12,9 @@
 LANES = 128
 
 
-def fused_kernel(m, n, x_hbm, gwin_ref, w_ref, cot_ref, dx_hbm, wg_ref, gg_ref,
-                 x_ref, gbuf, gfull, wall, t_ref, pr, xs, xr, u_ref, zs, zr, sref, dxv,
-                 x_sem, dx_sem, g_send, g_recv, wz_send, wz_recv, wf_send, wf_recv,
+def fused_kernel(m, n, window, x_hbm, gain_ref, w_ref, cot_ref, dx_ref, wg_ref, gg_ref,
+                 x_ref, gwin_ref, gbuf, gfull, wall, t_ref, pr, xs, xr, u_ref, zs, zr, sref,
+                 x_sem, g_send, g_recv, wz_send, wz_recv, wf_send, wf_recv,
                  p_send, p_recv, x_send, x_recv, z_send, z_recv):
     a, j = lax.axis_index("inter"), lax.axis_index("intra")
     z, c = j // 2, lax.rem(j, 2)
@@ -23,7 +23,6 @@
     tokens, features = x_ref.shape
     quarter, pair, shard = features // m, features // chips, features // n
     block = quarter // n
-    window = gwin_ref.shape[1]
     low = pair - window
 
     barrier = pltpu.get_barrier_semaphore()
@@ -33,8 +32,20 @@
         pl.semaphore_signal(barrier, inc=1, device_id=(lax.rem(a + k, m), j), device_id_type=MESH)
     x_copy = pltpu.make_async_copy(x_hbm, x_ref, x_sem)
     x_copy.start()
+    own_gain = gain_ref[...].astype(jnp.float32).reshape(1, shard)
+    blank = jnp.zeros((1, window - shard), jnp.float32)
+    gwin_ref[...] = jnp.where(c == 1, jnp.concatenate([blank, own_gain], axis=1),
+                              jnp.concatenate([own_gain, blank], axis=1))
     gbuf[j] = gwin_ref[...]
     wall[pl.ds(pl.multiple_of(j * shard, 16), shard), :] = w_ref[...]
+    x_copy.wait()
+    wide = x_ref[...].astype(jnp.float32)
+    inv = lax.rsqrt(jnp.mean(wide * wide, axis=1, keepdims=True) + EPS)
+    scaled_cot = cot_ref[...].astype(jnp.float32) * inv
+    high = scaled_cot.astype(jnp.bfloat16)
+    low_half = (scaled_cot - high.astype(jnp.float32)).astype(jnp.bfloat16)
+    halves = jnp.concatenate([high, low_half], axis=1)
+    width = cot_ref.shape[1]
     pl.semaphore_wait(barrier, n - 1 + m - 1)
 
     def send(src, dst, s_sem, r_sem, to):
@@ -57,19 +68,6 @@
         to = lax.rem(z + k, chips)
         w_z.append(send(w_ref, rows_of(j), wz_send.at[k - 1], wz_recv.at[k - 1], (a, 2 * to + c)))
     w_f = [send(w_ref, rows_of(j), wf_send.at[0], wf_recv.at[0], mate)]
-
-    x_copy.wait()
-    wide = x_ref[...].astype(jnp.float32)
-    inv = lax.rsqrt(jnp.mean(wide * wide, axis=1, keepdims=True) + EPS)
-
-    for copy in gains:
-        copy.wait_recv()
-    for q in range(chips):
-        even, odd = gbuf[2 * q], gbuf[2 * q + 1]
-        base = q * pair
-        gfull[:, base:base + low] = even[:, :low]
-        gfull[:, base + low:base + window] = even[:, low:] + odd[:, :window - low]
-        gfull[:, base + window:base + pair] = odd[:, window - low:]
 
     order = list(range(1, m)) + [0]
     p_copies, x_copies = {}, []
@@ -78,9 +76,9 @@
             k = order[step]
             part = lax.rem(a + k, m)
             cols = pl.ds(pl.multiple_of(part * quarter, LANES), quarter)
-            normed = (x_ref[:, cols].astype(jnp.float32) * inv * gfull[:, cols]).astype(jnp.bfloat16)
-            term = lax.dot_general(normed, cot_ref[...], (((0,), (0,)), ((), ())),
+            both = lax.dot_general(x_ref[:, cols], halves, (((0,), (0,)), ((), ())),
                                    preferred_element_type=jnp.float32)
+            term = both[:, :width] + both[:, width:]
             for q in range(chips):
                 for core in range(2):
                     at = (2 * q + core) * block
@@ -96,6 +94,15 @@
             else:
                 u_ref[...] = t_ref[0, c] + pr[0]
 
+    for copy in gains:
+        copy.wait_recv()
+    for q in range(chips):
+        even, odd = gbuf[2 * q], gbuf[2 * q + 1]
+        base = q * pair
+        gfull[:, base:base + low] = even[:, :low]
+        gfull[:, base + low:base + window] = even[:, low:] + odd[:, :window - low]
+        gfull[:, base + window:base + pair] = odd[:, window - low:]
+
     for k in range(1, chips):
         w_z[k - 1].wait_recv()
         owner = 2 * lax.rem(z - k + chips, chips) + c
@@ -130,20 +137,16 @@
     for k in range(chips):
         acc = feature(k, acc)
     centre = acc * (1.0 / features)
-    dx_copies = []
     for q in range(m):
         cols = slice(q * quarter, (q + 1) * quarter)
         normal = x_ref[:, cols].astype(jnp.float32) * inv
-        dxv[:, cols] = (inv * (sref[:, cols] - normal * centre)).astype(jnp.bfloat16)
-        copy = pltpu.make_async_copy(dxv.at[:, cols], dx_hbm.at[:, cols], dx_sem.at[q])
-        copy.start()
-        dx_copies.append(copy)
+        dx_ref[:, cols] = (inv * (sref[:, cols] - normal * centre)).astype(jnp.bfloat16)
 
     cols = pl.ds(pl.multiple_of(a * quarter, LANES), quarter)
     lane = lax.broadcasted_iota(jnp.int32, (block, quarter), 1)
     row = lax.broadcasted_iota(jnp.int32, (block, quarter), 0)
     gain = jnp.sum(jnp.where(lane == row + j * block, gfull[:, cols], 0.0), axis=1, keepdims=True)
-    own = wall[pl.ds(pl.multiple_of((a * n + j) * block, 16), block), :].astype(jnp.float32) / gain
+    own = wall[pl.ds(pl.multiple_of((a * n + j) * block, 16), block), :].astype(jnp.float32)
 
     for copy in z_copies:
         copy.wait_recv()
@@ -151,14 +154,12 @@
     for k in range(1, chips):
         final = final + zr[k - 1].astype(jnp.float32)
     final = final / float(m * n)
-    wg_ref[...] = final
+    wg_ref[...] = final * gain
     ones = jnp.ones((8, final.shape[1]), jnp.float32)
     sums = lax.dot_general(ones, final * own, (((1,), (1,)), ((), ())),
                            precision=lax.Precision.HIGHEST, preferred_element_type=jnp.float32)
     gg_ref[...] = sums[0:1, :]
 
-    for copy in dx_copies:
-        copy.wait()
     for copy in gains + w_z + w_f + list(p_copies.values()) + x_copies + z_copies:
         copy.wait_send()
 
@@ -173,25 +174,22 @@
     block = features // (m * n)
     half = features // m // 2
     window = pair - shard // LANES * LANES
-    lead = window - shard
-    wide = norm_gain.astype(jnp.float32)
-    odd = lax.rem(lax.axis_index("intra"), 2) == 1
-    gwin = jnp.where(odd, jnp.pad(wide, (lead, 0)), jnp.pad(wide, (0, lead))).reshape(1, window)
     f32, bf16 = jnp.float32, jnp.bfloat16
     dma = pltpu.SemaphoreType.DMA
     vmem = pl.BlockSpec(memory_space=pltpu.VMEM)
-    hbm = pl.BlockSpec(memory_space=pl.ANY)
+    hbm = pl.BlockSpec(memory_space=pltpu.HBM)
     dx, wg, gg = pl.pallas_call(
-        functools.partial(fused_kernel, m, n),
+        functools.partial(fused_kernel, m, n, window),
         out_shape=(
             jax.ShapeDtypeStruct((tokens, features), bf16),
             jax.ShapeDtypeStruct((block, width), f32),
             jax.ShapeDtypeStruct((1, block), f32),
         ),
         in_specs=[hbm, vmem, vmem, vmem],
-        out_specs=(hbm, vmem, vmem),
+        out_specs=(vmem, vmem, vmem),
         scratch_shapes=[
             pltpu.VMEM((tokens, features), bf16),
+            pltpu.VMEM((1, window), f32),
             pltpu.VMEM((n, 1, window), f32),
             pltpu.VMEM((1, features), f32),
             pltpu.VMEM((features, width), bf16),
@@ -203,8 +201,7 @@
             pltpu.VMEM((chips - 1, block, width), bf16),
             pltpu.VMEM((chips - 1, block, width), bf16),
             pltpu.VMEM((tokens, features), f32),
-            pltpu.VMEM((tokens, features), bf16),
-            dma(()), dma((m,)),
+            dma(()),
             dma((n - 1,)), dma((n - 1,)),
             dma((chips - 1,)), dma((chips - 1,)),
             dma((chips,)), dma((chips,)),
@@ -212,8 +209,8 @@
             dma((m - 1,)), dma((m - 1,)),
             dma((chips - 1,)), dma((chips - 1,)),
         ],
-        compiler_params=pltpu.CompilerParams(collective_id=0, has_side_effects=True),
-    )(layer_input, gwin, kv_weight, kv_cotangent)
+        compiler_params=pltpu.CompilerParams(collective_id=0, has_side_effects=True, vmem_limit_bytes=24 * 2**20),
+    )(layer_input, norm_gain, kv_weight, kv_cotangent)
     return dx, wg, gg.reshape(block)
 
 

time: 34.6 us -> 32.5 us (0.939)
  Pallas kernels: 28.8 us -> 25.8 us
  local copies, waits for them, and re-layouts: 4.18 us -> 5.82 us
  other arithmetic: 0.76 us -> 0 us
    pallas_call x1, Pallas kernels: 28.8 us -> 25.8 us  [fused(): pl.pallas_call(functools.partial(fused_kernel, m, n, window), out_shape=(...]
    unnamed x7 -> x11, local copies, waits for them, and re-layouts: 3.59 us -> 5.82 us
    convert_element_type x1 -> x0, other arithmetic: 0.68 us -> none  [fused(): wide = norm_gain.astype(jnp.float32)]
    reshape x1 -> x0, local copies, waits for them, and re-layouts: 0.58 us -> none  [fused(): jnp.where(odd, jnp.pad(wide, (lead, 0)), jnp.pad(wide, (0, lead)))]
where the time goes in v2:
time: 32.5 us; the launch traced here: 32.2 us
  Pallas kernels  25.8 us (79%)
  local copies, waits for them, and re-layouts  5.82 us (18%)
  between operations  0.65 us (2%)
    pallas_call x1, Pallas kernels, fused(): pl.pallas_call(functools.partial(fused_kernel, m, n, window), out_shape=(...  25.8 us
    unnamed x11, local copies, waits for them, and re-layouts  5.82 us

profile of v2, /device:TPU:0, one launch (start us, length us, event | category | flops | bytes accessed | tf_op | source)
XLA Modules:
  0.0 32.2 jit_solution(196210839457030080)
XLA Ops:
  0.6 0.0 copy-start
  0.6 1.3 %copy-done = bf16[128,4608]{1,0:T(8,128)(2,1)S(1)} copy-done((bf16[128,4608]{1,0:T(8,128)(2,1)S(1)}, bf16[128,4608]{1,0:T(8,128)(2,1)}, u32[]{:S(2)}) %copy-start) | copy-done | bytes 1179672
  1.9 0.0 copy-start.1
  1.9 0.9 %copy-done.1 = bf16[576,128]{1,0:T(8,128)(2,1)S(1)} copy-done((bf16[576,128]{1,0:T(8,128)(2,1)S(1)}, bf16[576,128]{1,0:T(8,128)(2,1)}, u32[]{:S(2)}) %copy-start.1) | copy-done | bytes 147480
  2.8 0.0 copy-start.2
  2.8 0.8 %copy-done.2 = bf16[128,128]{1,0:T(8,128)(2,1)S(1)} copy-done((bf16[128,128]{1,0:T(8,128)(2,1)S(1)}, bf16[128,128]{1,0:T(8,128)(2,1)}, u32[]{:S(2)}) %copy-start.2) | copy-done | bytes 32792
  3.6 0.0 copy-start.3
  3.6 0.7 %copy-done.3 = bf16[576]{0:T(1024)(128)(2,1)S(1)} copy-done((bf16[576]{0:T(1024)(128)(2,1)S(1)}, bf16[576]{0:T(1024)(128)(2,1)}, u32[]{:S(2)}) %copy-start.3) | copy-done | bytes 1176
  4.3 25.8 %shard_map.67 = (bf16[128,4608]{1,0:T(8,128)(2,1)S(1)}, f32[144,128]{1,0:T(8,128)S(1)}, f32[1,144]{1,0:T(1,128)S(1)}) custom-call(bf16[128,4608]{1,0:T(8,128)(2,1)S(1)} %copy-done, bf16[576]{0:T(1024)(128)(2,1)S(1)} %copy-done.3, bf16[576,128]{1,0:T(8,128)(2,1)S(1)} %copy-done.1, bf16[128,128]{1,0:T(8,128)(2,1)S(1)} %copy-done.2), custom_call_target="tpu_custom_call" | custom-call | tf_op jit(solution)/shard_map/pallas_call | solution.py:181
  30.0 1.0 %copy.10 = bf16[128,4608]{1,0:T(8,128)(2,1)} copy(bf16[128,4608]{1,0:T(8,128)(2,1)S(1)} %get-tuple-element.12) | data formatting | bytes 2359296
  31.0 0.6 %copy.11 = f32[144,128]{1,0:T(8,128)} copy(f32[144,128]{1,0:T(8,128)S(1)} %get-tuple-element.13) | data formatting | bytes 147456
  31.7 0.6 %copy.12 = f32[144]{0:T(256)} copy(f32[144]{0:T(256)S(1)} %bitcast.1) | data formatting | bytes 1152
Async XLA Ops:
  0.6 1.3 %copy-start = (bf16[128,4608]{1,0:T(8,128)(2,1)S(1)}, bf16[128,4608]{1,0:T(8,128)(2,1)}, u32[]{:S(2)}) copy-start(bf16[128,4608]{1,0:T(8,128)(2,1)} %x_hbm.1) | copy-start | bytes 3538948
  1.9 0.9 %copy-start.1 = (bf16[576,128]{1,0:T(8,128)(2,1)S(1)}, bf16[576,128]{1,0:T(8,128)(2,1)}, u32[]{:S(2)}) copy-start(bf16[576,128]{1,0:T(8,128)(2,1)} %w_ref.1) | copy-start | bytes 442372
  2.8 0.8 %copy-start.2 = (bf16[128,128]{1,0:T(8,128)(2,1)S(1)}, bf16[128,128]{1,0:T(8,128)(2,1)}, u32[]{:S(2)}) copy-start(bf16[128,128]{1,0:T(8,128)(2,1)} %cot_ref.1) | copy-start | bytes 98308
  3.6 0.7 %copy-start.3 = (bf16[576]{0:T(1024)(128)(2,1)S(1)}, bf16[576]{0:T(1024)(128)(2,1)}, u32[]{:S(2)}) copy-start(bf16[576]{0:T(1024)(128)(2,1)} %gain_ref.1) | copy-start | bytes 3460

commit v3 on v2

--- a/solution.py
+++ b/solution.py
@@ -10,11 +10,12 @@
 EPS = 1e-05
 MESH = pl.DeviceIdType.MESH
 LANES = 128
+HALVES = 2
 
 
 def fused_kernel(m, n, window, x_hbm, gain_ref, w_ref, cot_ref, dx_ref, wg_ref, gg_ref,
                  x_ref, gwin_ref, gbuf, gfull, wall, t_ref, pr, xs, xr, u_ref, zs, zr, sref,
-                 x_sem, g_send, g_recv, wz_send, wz_recv, wf_send, wf_recv,
+                 x_sem, g_send, g_recv, wr_send, wl_send, wz_recv, wf_send, wf_recv,
                  p_send, p_recv, x_send, x_recv, z_send, z_recv):
     a, j = lax.axis_index("inter"), lax.axis_index("intra")
     z, c = j // 2, lax.rem(j, 2)
@@ -59,15 +60,61 @@
     for k in range(1, n):
         gains.append(send(gwin_ref, gbuf.at[j], g_send.at[k - 1], g_recv.at[k - 1], (a, lax.rem(j + k, n))))
 
-    def rows_of(owner):
-        return wall.at[pl.ds(pl.multiple_of(owner * shard, 16), shard), :]
+    piece = shard // HALVES
+
+    def piece_of(chip, core, h):
+        return wall.at[pl.ds(pl.multiple_of((2 * chip + core) * shard + h * piece, 16), piece), :]
 
     mate = (a, 2 * z + other)
-    w_z = []
-    for k in range(1, chips):
-        to = lax.rem(z + k, chips)
-        w_z.append(send(w_ref, rows_of(j), wz_send.at[k - 1], wz_recv.at[k - 1], (a, 2 * to + c)))
-    w_f = [send(w_ref, rows_of(j), wf_send.at[0], wf_recv.at[0], mate)]
+
+    def remote(src, dst, s_sem, r_sem, to):
+        return pltpu.make_async_remote_copy(src_ref=src, dst_ref=dst, send_sem=s_sem, recv_sem=r_sem,
+                                            device_id=to, device_id_type=MESH)
+
+    def along(chip, h, up, d):
+        sems, step = (wr_send, 1) if up else (wl_send, -1)
+        to = lax.rem(z + step + chips, chips)
+        part = piece_of(chip, c, h)
+        src = part if d else w_ref.at[pl.ds(h * piece, piece), :]
+        return remote(src, part, sems.at[chip, h], wz_recv.at[chip, h], (a, 2 * to + c))
+
+    def across(chip, h, core, d):
+        part = piece_of(chip, core, h)
+        src = part if d else w_ref.at[pl.ds(h * piece, piece), :]
+        return remote(src, part, wf_send.at[chip, h], wf_recv.at[chip, h], mate)
+
+    def relay(d):
+        for h in range(HALVES):
+            for up in (True, False):
+                chip = z - d if up else z + d
+
+                @pl.when(chip >= 0 if up else chip < chips)
+                def _():
+                    if d:
+                        along(chip, h, up, d).wait_recv()
+
+                    @pl.when(z < chips - 1 if up else z > 0)
+                    def _():
+                        along(chip, h, up, d).start()
+
+                    if d or up:
+                        across(chip, h, c, d).start()
+
+    def settle(d):
+        for h in range(HALVES):
+            for up in (True, False):
+                chip = z - d if up else z + d
+
+                @pl.when(chip >= 0 if up else chip < chips)
+                def _():
+                    @pl.when(z < chips - 1 if up else z > 0)
+                    def _():
+                        along(chip, h, up, d).wait_send()
+
+                    if d or up:
+                        across(chip, h, c, d).wait_send()
+
+    relay(0)
 
     order = list(range(1, m)) + [0]
     p_copies, x_copies = {}, []
@@ -103,16 +150,14 @@
         gfull[:, base + low:base + window] = even[:, low:] + odd[:, :window - low]
         gfull[:, base + window:base + pair] = odd[:, window - low:]
 
-    for k in range(1, chips):
-        w_z[k - 1].wait_recv()
-        owner = 2 * lax.rem(z - k + chips, chips) + c
-        w_f.append(send(rows_of(owner), rows_of(owner), wf_send.at[k], wf_recv.at[k], mate))
+    relay(1)
 
     acc = jnp.zeros((tokens, 1), jnp.float32)
 
     def feature(k, acc):
-        w_f[k].wait_recv()
-        q = lax.rem(z - k + chips, chips)
+        q = lax.rem(z + (1 - 2 * (2 * z // chips)) * k + chips, chips)
+        for h in range(HALVES):
+            across(q, h, other, 1).wait_recv()
         cols = pl.ds(pl.multiple_of(q * pair, LANES), pair)
         grad = lax.dot_general(cot_ref[...], wall[cols, :], (((1,), (1,)), ((), ())),
                                preferred_element_type=jnp.float32)
@@ -120,6 +165,11 @@
         sref[:, cols] = scaled
         normal = x_ref[:, cols].astype(jnp.float32) * inv
         return acc + jnp.sum(scaled * normal, axis=1, keepdims=True)
+
+    acc = feature(0, acc)
+    for d in range(2, chips - 1):
+        relay(d)
+    acc = feature(1, acc)
 
     for copy in x_copies:
         copy.wait_recv()
@@ -134,7 +184,8 @@
         zs[k - 1] = u_ref[rows, :].astype(jnp.bfloat16)
         z_copies.append(send(zs.at[k - 1], zr.at[k - 1], z_send.at[k - 1], z_recv.at[k - 1], (a, 2 * to + c)))
 
-    for k in range(chips):
+    relay(chips - 1)
+    for k in range(2, chips):
         acc = feature(k, acc)
     centre = acc * (1.0 / features)
     for q in range(m):
@@ -160,8 +211,10 @@
                            precision=lax.Precision.HIGHEST, preferred_element_type=jnp.float32)
     gg_ref[...] = sums[0:1, :]
 
-    for copy in gains + w_z + w_f + list(p_copies.values()) + x_copies + z_copies:
+    for copy in gains + list(p_copies.values()) + x_copies + z_copies:
         copy.wait_send()
+    for d in range(chips):
+        settle(d)
 
 
 def fused(layer_input, norm_gain, kv_weight, kv_cotangent):
@@ -203,14 +256,14 @@
             pltpu.VMEM((tokens, features), f32),
             dma(()),
             dma((n - 1,)), dma((n - 1,)),
-            dma((chips - 1,)), dma((chips - 1,)),
-            dma((chips,)), dma((chips,)),
+            dma((chips, HALVES)), dma((chips, HALVES)), dma((chips, HALVES)),
+            dma((chips, HALVES)), dma((chips, HALVES)),
             dma((m,)), dma((m,)),
             dma((m - 1,)), dma((m - 1,)),
             dma((chips - 1,)), dma((chips - 1,)),
         ],
         compiler_params=pltpu.CompilerParams(collective_id=0, has_side_effects=True, vmem_limit_bytes=24 * 2**20),
-    )(layer_input, norm_gain, kv_weight, kv_cotangent)
+    )(*(pltpu.with_memory_space_constraint(v, pltpu.HBM) for v in (layer_input, norm_gain, kv_weight, kv_cotangent)))
     return dx, wg, gg.reshape(block)
 
 
@@ -252,7 +305,8 @@
     m, n = lax.axis_size("inter"), lax.axis_size("intra")
     features = layer_input.shape[1]
     fits = (
-        n % 2 == 0 and n > 2 and m > 1
+        n % 2 == 0 and n > 4 and m > 1
+        and kv_weight.shape[0] % (16 * HALVES) == 0
         and features % (16 * m * n) == 0
         and features % (LANES * m) == 0
         and 2 * features % (LANES * n) == 0

time: 32.5 us -> 25.5 us (0.78)
  local copies, waits for them, and re-layouts: 5.82 us -> 2.21 us
  Pallas kernels: 25.8 us -> 22.5 us
    unnamed x11 -> x3, local copies, waits for them, and re-layouts: 5.82 us -> 2.21 us
    pallas_call x1, Pallas kernels: 25.8 us -> 22.5 us  [fused(): pl.pallas_call(functools.partial(fused_kernel, m, n, window), out_shape=(...]
where the time goes in v3:
time: 25.5 us; the launch traced here: 25.3 us
  Pallas kernels  22.5 us (88%)
  local copies, waits for them, and re-layouts  2.21 us (9%)
  between operations  0.64 us (3%)
    pallas_call x1, Pallas kernels, fused(): pl.pallas_call(functools.partial(fused_kernel, m, n, window), out_shape=(...  22.5 us
    unnamed x3, local copies, waits for them, and re-layouts  2.21 us

profile of v3, /device:TPU:0, one launch (start us, length us, event | category | flops | bytes accessed | tf_op | source)
XLA Modules:
  0.0 25.3 jit_solution(8445844388557369302)
XLA Ops:
  0.6 22.5 %shard_map.67 = (bf16[128,4608]{1,0:T(8,128)(2,1)S(1)}, f32[144,128]{1,0:T(8,128)S(1)}, f32[1,144]{1,0:T(1,128)S(1)}) custom-call(bf16[128,4608]{1,0:T(8,128)(2,1)} %x_hbm.1, bf16[576]{0:T(1024)(128)(2,1)} %gain_ref.1, bf16[576,128]{1,0:T(8,128)(2,1)} %w_ref.1, bf16[128,128]{1,0:T(8,128)(2,1)} %cot_ref.1), custom_call_target="tpu_custom_call" | custom-call | tf_op jit(solution)/shard_map/pallas_call | solution.py:234
  23.1 1.0 %copy.10 = bf16[128,4608]{1,0:T(8,128)(2,1)} copy(bf16[128,4608]{1,0:T(8,128)(2,1)S(1)} %get-tuple-element.12) | data formatting | bytes 2359296
  24.1 0.6 %copy.11 = f32[144,128]{1,0:T(8,128)} copy(f32[144,128]{1,0:T(8,128)S(1)} %get-tuple-element.13) | data formatting | bytes 147456
  24.8 0.6 %copy.12 = f32[144]{0:T(256)} copy(f32[144]{0:T(256)S(1)} %bitcast.1) | data formatting | bytes 1152

commit v4 on v3

--- a/solution.py
+++ b/solution.py
@@ -215,6 +215,15 @@
         copy.wait_send()
     for d in range(chips):
         settle(d)
+
+
+def write_kernel(*refs):
+    sources, results, sems = refs[:3], refs[3:6], refs[6]
+    copies = [pltpu.make_async_copy(sources[i], results[i], sems.at[i]) for i in range(3)]
+    for copy in copies:
+        copy.start()
+    for copy in copies:
+        copy.wait()
 
 
 def fused(layer_input, norm_gain, kv_weight, kv_cotangent):
@@ -264,6 +273,14 @@
         ],
         compiler_params=pltpu.CompilerParams(collective_id=0, has_side_effects=True, vmem_limit_bytes=24 * 2**20),
     )(*(pltpu.with_memory_space_constraint(v, pltpu.HBM) for v in (layer_input, norm_gain, kv_weight, kv_cotangent)))
+    dx, wg, gg = pl.pallas_call(
+        write_kernel,
+        out_shape=tuple(jax.ShapeDtypeStruct(v.shape, v.dtype) for v in (dx, wg, gg)),
+        in_specs=[vmem] * 3,
+        out_specs=(hbm,) * 3,
+        scratch_shapes=[dma((3,))],
+        compiler_params=pltpu.CompilerParams(vmem_limit_bytes=8 * 2**20),
+    )(dx, wg, gg)
     return dx, wg, gg.reshape(block)
 
 

time: 25.5 us -> 24.3 us (0.953)
  local copies, waits for them, and re-layouts: 2.21 us -> 0 us
  Pallas kernels: 22.5 us -> 23.5 us
    unnamed x3 -> x0, local copies, waits for them, and re-layouts: 2.21 us -> none
    pallas_call x0 -> x1, Pallas kernels: none -> 1.05 us  [fused(): pl.pallas_call(write_kernel, out_shape=tuple((jax.ShapeDtypeStruct(v.shap...]
where the time goes in v4:
time: 24.3 us; the launch traced here: 24.2 us
  Pallas kernels  23.5 us (97%)
  between operations  0.64 us (3%)
    pallas_call x1, Pallas kernels, fused(): pl.pallas_call(functools.partial(fused_kernel, m, n, window), out_shape=(...  22.5 us
    pallas_call x1, Pallas kernels, fused(): pl.pallas_call(write_kernel, out_shape=tuple((jax.ShapeDtypeStruct(v.shap...  1.05 us

profile of v4, /device:TPU:0, one launch (start us, length us, event | category | flops | bytes accessed | tf_op | source)
XLA Modules:
  0.0 24.2 jit_solution(2078135122168543686)
XLA Ops:
  0.6 22.5 %shard_map.67 = (bf16[128,4608]{1,0:T(8,128)(2,1)S(1)}, f32[144,128]{1,0:T(8,128)S(1)}, f32[1,144]{1,0:T(1,128)S(1)}) custom-call(bf16[128,4608]{1,0:T(8,128)(2,1)} %x_hbm.1, bf16[576]{0:T(1024)(128)(2,1)} %gain_ref.1, bf16[576,128]{1,0:T(8,128)(2,1)} %w_ref.1, bf16[128,128]{1,0:T(8,128)(2,1)} %cot_ref.1), custom_call_target="tpu_custom_call" | custom-call | tf_op jit(solution)/shard_map/pallas_call | solution.py:243
  23.1 1.1 %shard_map.68 = (bf16[128,4608]{1,0:T(8,128)(2,1)}, f32[144,128]{1,0:T(8,128)}, f32[1,144]{1,0:T(1,128)}) custom-call(bf16[128,4608]{1,0:T(8,128)(2,1)S(1)} %get-tuple-element.9.refs_0_, f32[144,128]{1,0:T(8,128)S(1)} %get-tuple-element.10.refs_1_, f32[1,144]{1,0:T(1,128)S(1)} %get-tuple-element.11.refs_2_), custom_call_target="tpu_custom_call" | custom-call | tf_op jit(solution)/shard_map/pallas_call | solution.py:276
